TPU v7x, 32 devices: a whole 2x2x4 slice. The times are simulated.
32 devices in a mesh: seq: 8 (over z, y), mp: 4 (over x, core).
Axes of the slice: x: 2, y: 2, z: 4, core: 2. Of those that a mesh axis runs over, the one named last changes fastest.
Arguments:
- hidden_in: bfloat16 [2, 1024, 2048], P(None, 'seq'), may hold values from -6 to 6
- attn_gain: float32 [2048], replicated, may hold values from 0.1 to 1.9
- q_weight: bfloat16 [2048, 2048], P(None, 'mp'), may hold values from -0.125 to 0.125
- q_bias: float32 [2048], P('mp'), may hold values from -60 to 60
- k_weight: bfloat16 [2048, 256], replicated, may hold values from -0.125 to 0.125
- k_bias: float32 [256], replicated, may hold values from -60 to 60
- v_weight: bfloat16 [2048, 256], replicated, may hold values from -0.125 to 0.125
- v_bias: float32 [256], replicated, may hold values from -3 to 3
- o_weight: bfloat16 [2048, 2048], P('mp'), may hold values from -0.125 to 0.125
- mlp_gain: float32 [2048], replicated, may hold values from 0.1 to 1.9
- gate_weight: bfloat16 [2048, 5632], P('seq', 'mp'), may hold values from -0.125 to 0.125
- up_weight: bfloat16 [2048, 5632], P('seq', 'mp'), may hold values from -0.125 to 0.125
- down_weight: bfloat16 [2048, 5632], P('seq', 'mp'), may hold values from -0.078125 to 0.078125
- lengths: int32 [2], replicated, may hold values from 512 to 1024
Outputs:
- layer_out: bfloat16 [2, 1024, 2048], P(None, 'seq', 'mp')
- influence: float32 [2, 1024], P(None, 'seq')
- score: float32 [2], replicated
Inputs may be any that keep to these rules, and one draw needn't show every extreme that they name: `lengths`: tokens at positions 512 and later may be invalid.
All inputs are finite; a program needn't handle non-finite values.
Results may differ from a plain program's by a relative error of at most 0.02.
The roundings to bfloat16 on the way count: a program that leaves them out, or rounds other values in their place, can miss the bound.
Values may be sent and summed in bfloat16 or wider, within the bound.
A program may use at most 192 MiB of HBM per device.

v0:
```python
import jax
import jax.numpy as jnp
from jax import lax
from jax.sharding import PartitionSpec as P

HEADS = 16
KV_HEADS = 2
HEAD = 128
rope_base = 1000000.0
norm_eps = 1e-06
masked_score = -1e30


def rms_scale(values, gain):
    widened = values.astype(jnp.float32)
    factor = lax.rsqrt(jnp.mean(widened * widened, axis=-1, keepdims=True) + norm_eps)
    return (widened * factor * gain).astype(jnp.bfloat16)


def rotate(values, positions):
    head_width = values.shape[-1]
    half_width = head_width // 2
    inv_freq = rope_base ** (-(jnp.arange(half_width, dtype=jnp.float32) * 2.0) / head_width)
    angles = positions.astype(jnp.float32)[:, None] * inv_freq[None, :]
    angles = jnp.concatenate([angles, angles], axis=-1)
    first_part = values[..., :half_width]
    second_part = values[..., half_width:]
    turned = jnp.concatenate([-second_part, first_part], axis=-1)
    return values * jnp.cos(angles) + turned * jnp.sin(angles)


def attend_update(state, queries, first_pos, key_piece, value_piece):
    run_max, run_sum, run_acc = state
    score_scale = queries.shape[-1] ** (-0.5)
    query_pos = first_pos + jnp.arange(queries.shape[2], dtype=jnp.int32)
    key_pos = jnp.arange(key_piece.shape[1], dtype=jnp.int32)
    scores = (
        jnp.einsum("shqd,skd->shqk", queries, key_piece, preferred_element_type=jnp.float32)
        * score_scale
    )
    allowed = key_pos[None, :] <= query_pos[:, None]
    scores = jnp.where(allowed, scores, masked_score)
    new_max = jnp.maximum(run_max, jnp.max(scores, axis=-1))
    weights = jnp.where(allowed, jnp.exp(scores - new_max[..., None]), 0.0)
    new_sum = jnp.sum(weights, axis=-1)
    mixed = jnp.einsum(
        "shqk,skd->shqd",
        weights.astype(jnp.bfloat16),
        value_piece,
        preferred_element_type=jnp.float32,
    )
    return (new_max, new_sum, mixed)


def local(
    hidden_in,
    attn_gain,
    q_weight,
    q_bias,
    k_weight,
    k_bias,
    v_weight,
    v_bias,
    o_weight,
    mlp_gain,
    gate_weight,
    up_weight,
    down_weight,
    lengths,
):
    seqs_n, tok_n, width = hidden_in.shape
    seq_rank = lax.axis_index("seq")
    mp_devices = lax.axis_size("mp")
    mp_rank = lax.axis_index("mp")
    heads_here = q_weight.shape[1] // HEAD
    group_size = HEADS // KV_HEADS
    kv_index = mp_rank * heads_here // group_size
    flat_in = hidden_in.reshape(seqs_n * tok_n, width)
    normed = rms_scale(flat_in, attn_gain)
    query_all = jnp.dot(normed, q_weight, preferred_element_type=jnp.float32) + q_bias
    key_cols = lax.dynamic_slice_in_dim(k_weight, kv_index * HEAD, HEAD, 1)
    value_cols = lax.dynamic_slice_in_dim(v_weight, kv_index * HEAD, HEAD, 1)
    key_shift = lax.dynamic_slice_in_dim(k_bias, kv_index * HEAD, HEAD, 0)
    value_shift = lax.dynamic_slice_in_dim(v_bias, kv_index * HEAD, HEAD, 0)
    key_all = jnp.dot(normed, key_cols, preferred_element_type=jnp.float32) + key_shift
    value_rows = (
        jnp.dot(normed, value_cols, preferred_element_type=jnp.float32) + value_shift
    ).astype(jnp.bfloat16)
    positions = seq_rank * tok_n + jnp.arange(tok_n, dtype=jnp.int32)
    rotated_q = rotate(
        query_all.reshape(seqs_n, tok_n, heads_here, HEAD).transpose(0, 2, 1, 3), positions
    ).astype(jnp.bfloat16)
    rotated_k = rotate(key_all.reshape(seqs_n, tok_n, HEAD), positions).astype(jnp.bfloat16)
    value_rows = value_rows.reshape(seqs_n, tok_n, HEAD)
    query_sets = ((rotated_q, seq_rank * tok_n),)
    initial = tuple(
        (
            (
                jnp.full(entry[0].shape[:3], masked_score, jnp.float32),
                jnp.zeros(entry[0].shape[:3], jnp.float32),
                jnp.zeros(entry[0].shape, jnp.float32),
            )
            for entry in query_sets
        )
    )
    key_start = jnp.int32(0)
    key_piece = lax.all_gather(rotated_k, "seq", axis=1, tiled=True)
    value_piece = lax.all_gather(value_rows, "seq", axis=1, tiled=True)
    updated = []
    for state, query_entry in zip(initial, query_sets):
        queries, first_pos = query_entry
        last_pos = first_pos + queries.shape[2] - 1

        def run_update(current):
            return attend_update(current, queries, first_pos, key_piece, value_piece)

        def keep_state(current):
            return current

        updated.append(lax.cond(key_start <= last_pos, run_update, keep_state, state))
    results = tuple(updated)
    finished = [(entry[2] / entry[1][..., None]).astype(jnp.bfloat16) for entry in results]
    attn = finished[0]
    attn = attn.transpose(0, 2, 1, 3).reshape(seqs_n * tok_n, heads_here * HEAD)
    projected = jnp.dot(attn, o_weight, preferred_element_type=jnp.float32)
    quarter = width // mp_devices
    own_in = lax.dynamic_slice_in_dim(flat_in, mp_rank * quarter, quarter, 1)
    summed = lax.psum(projected.astype(jnp.bfloat16), "mp").astype(jnp.float32)
    residual = (flat_in.astype(jnp.float32) + summed).astype(jnp.bfloat16)
    resid_part = lax.dynamic_slice_in_dim(residual, mp_rank * quarter, quarter, 1)
    mlp_in = rms_scale(residual, mlp_gain)
    gate_sum = jnp.dot(
        mlp_in,
        lax.all_gather(gate_weight, "seq", axis=0, tiled=True),
        preferred_element_type=jnp.float32,
    )
    up_sum = jnp.dot(
        mlp_in,
        lax.all_gather(up_weight, "seq", axis=0, tiled=True),
        preferred_element_type=jnp.float32,
    )
    activated = (jax.nn.silu(gate_sum) * up_sum).astype(jnp.bfloat16)
    down_part = lax.dot_general(
        activated,
        lax.all_gather(down_weight, "seq", axis=0, tiled=True),
        (((1,), (1,)), ((), ())),
        preferred_element_type=jnp.float32,
    )
    mlp_share = lax.psum_scatter(
        down_part.astype(jnp.bfloat16), "mp", scatter_dimension=1, tiled=True
    ).astype(jnp.float32)
    layer_part = (resid_part.astype(jnp.float32) + mlp_share).astype(jnp.bfloat16)
    in_share = own_in.astype(jnp.float32)
    out_share = layer_part.astype(jnp.float32)
    cross_part = jnp.sum(in_share * out_share, axis=-1).reshape(seqs_n, tok_n)
    out_part = jnp.sum(out_share * out_share, axis=-1).reshape(seqs_n, tok_n)
    cross, out_norm = lax.psum((cross_part, out_part), "mp")
    in_wide = flat_in.astype(jnp.float32)
    in_norm = jnp.sum(in_wide * in_wide, axis=-1).reshape(seqs_n, tok_n)
    cosine = cross / jnp.sqrt((in_norm + norm_eps) * (out_norm + norm_eps))
    valid = positions[None, :] < lengths[:, None]
    influence = jnp.where(valid, 1.0 - cosine, 0.0)
    seq_total = lax.psum(jnp.sum(influence, axis=1), "seq")
    score = seq_total / lengths.astype(jnp.float32)
    return (layer_part.reshape(seqs_n, tok_n, quarter), influence, score)


def solution(mesh):
    placed = (
        P(None, "seq", None),
        P(),
        P(None, "mp"),
        P("mp"),
        P(),
        P(),
        P(),
        P(),
        P("mp", None),
        P(),
        P("seq", "mp"),
        P("seq", "mp"),
        P("seq", "mp"),
        P(),
    )
    return jax.shard_map(
        local,
        mesh=mesh,
        in_specs=placed,
        out_specs=(P(None, "seq", "mp"), P(None, "seq"), P()),
        check_vma=False,
    )
```

profile of v0, /device:TPU:0, one launch (start us, length us, event | category | flops | bytes accessed | tf_op | source)
XLA Modules:
  0.0 447.5 jit_solution(1680391220494171423)
XLA Ops:
  8.1 1.6 multiply_reduce_fusion
  10.6 1.5 fusion.14
  13.8 1.2 fusion.34
  15.0 35.3 %all_gather.15 = bf16[2,1024,128]{2,1,0:T(8,128)(2,1)} all-gather(bf16[2,128,128]{2,1,0:T(8,128)(2,1)S(1)} %fusion.34), channel_id=1, replica_groups=mesh['seq'=8,'mp'=4] {'seq'}, dimensions={1}, use_global_device_ids=true | all-gather | bytes 589824 | tf_op jit(solution)/shard_map/all_gather | solution.py:107
  50.3 1.5 fusion.19
  51.8 33.2 %all_gather.16 = bf16[2,1024,128]{2,1,0:T(8,128)(2,1)} all-gather(bf16[2,128,128]{2,1,0:T(8,128)(2,1)S(1)} %bitcast.49), channel_id=1, replica_groups=mesh['seq'=8,'mp'=4] {'seq'}, dimensions={1}, use_global_device_ids=true | all-gather | bytes 589824 | tf_op jit(solution)/shard_map/all_gather | solution.py:108
  85.0 1.5 convolution_add_fusion
  86.5 1.2 reshape.194
  87.8 1.2 slice_negate_fusion
  88.9 1.4 fusion.23
  90.4 3.7 conditional.1
  92.7 1.3 fusion.2
  94.5 1.7 convolution_convert_fusion
  98.2 35.9 %all-reduce.3.cloned.1.call-done = bf16[256,2048]{1,0:T(8,128)(2,1)} async-done(((bf16[256,2048]{1,0:T(8,128)(2,1)}), bf16[256,2048]{1,0:T(8,128)(2,1)}) %all-reduce.3.cloned.1.call-update) | async-done | bytes 1048592 | tf_op jit(solution)/shard_map/psum | solution.py:128
  134.1 2.6 fusion.16
  136.7 55.5 %all-gather.4.cloned.1.call-done = bf16[2048,1408]{1,0:T(8,128)(2,1)} async-done(((bf16[256,1408]{1,0:T(8,128)(2,1)}), bf16[2048,1408]{1,0:T(8,128)(2,1)}) %all-gather.4.cloned.1.call-update) | async-done | bytes 5767184 | tf_op jit(solution)/shard_map/all_gather | solution.py:134
  192.2 6.0 %fusion.28 = f32[256,1408]{1,0:T(8,128)} fusion(bf16[2048,1408]{1,0:T(8,128)(2,1)} %all-gather.4.cloned.1.call-done, bf16[256,2048]{1,0:T(8,128)(2,1)} %get-tuple-element.27, f32[2048]{0:T(1024)S(1)} %copy-done.7, f32[256]{0:T(256)S(1)} %add_rsqrt_fusion), kind=kOutput, calls=%fused_computation.48 | convolution fusion | flops 1478492160 | bytes 8266752 | tf_op jit(solution)/shard_map/dot_general | solution.py:132
  198.2 86.4 %all-gather.6.cloned.1.call-done = bf16[2048,1408]{1,0:T(8,128)(2,1)} async-done(((bf16[256,1408]{1,0:T(8,128)(2,1)}), bf16[2048,1408]{1,0:T(8,128)(2,1)}) %all-gather.6.cloned.1.call-update) | async-done | bytes 5767184 | tf_op jit(solution)/shard_map/all_gather | solution.py:139
  284.6 92.4 %all-gather.8.cloned.1.call-done = bf16[2048,1408]{1,0:T(8,128)(2,1)} async-done(((bf16[256,1408]{1,0:T(8,128)(2,1)}), bf16[2048,1408]{1,0:T(8,128)(2,1)}) %all-gather.8.cloned.1.call-update) | async-done | bytes 5767184 | tf_op jit(solution)/shard_map/all_gather | solution.py:145
  376.9 9.5 %convolution_convert_fusion.1 = bf16[256,2048]{1,0:T(8,128)(2,1)} fusion(bf16[2048,1408]{1,0:T(8,128)(2,1)} %all-gather.8.cloned.1.call-done, bf16[2048,1408]{1,0:T(8,128)(2,1)} %all-gather.6.cloned.1.call-done, f32[256,1408]{1,0:T(8,128)} %fusion.28, bf16[256,2048]{1,0:T(8,128)(2,1)} %get-tuple-element.27, f32[2048]{0:T(1024)S(1)} %copy-done.7, ...), kind=kOutput, calls=%fused_computation.23 | convolution fusion | flops 2957574144 | bytes 15082496 | tf_op jit(solution)/shard_map/dot_general | solution.py:143
  386.5 23.1 %reduce-scatter.2.cloned.1.call-done = bf16[256,512]{1,0:T(8,128)(2,1)} async-done(((bf16[256,2048]{1,0:T(8,128)(2,1)}), bf16[256,512]{1,0:T(8,128)(2,1)}) %reduce-scatter.2.cloned.1.call-update) | async-done | bytes 262160 | tf_op jit(solution)/shard_map/reduce_scatter | solution.py:149
  409.5 1.8 fusion.21
  411.4 5.7 %all-reduce = (f32[2,128]{1,0:T(2,128)S(1)}, f32[2,128]{1,0:T(2,128)S(1)}) all-reduce(f32[2,128]{1,0:T(2,128)S(1)} %bitcast.52, f32[2,128]{1,0:T(2,128)S(1)} %bitcast.51), channel_id=1, replica_groups=mesh['seq'=8,'mp'=4] {'mp'}, use_global_device_ids=true, to_apply=%region_9.10 | all-reduce | flops 512 | bytes 4096 | tf_op jit(solution)/shard_map/psum | solution.py:157
  417.8 21.5 %psum.31 = f32[2]{0:T(128)S(1)} all-reduce(f32[2]{0:T(128)S(1)} %get-tuple-element.23), channel_id=1, replica_groups=mesh['seq'=8,'mp'=4] {'seq'}, use_global_device_ids=true, to_apply=%region_13.14 | all-reduce | flops 2 | bytes 16 | tf_op jit(solution)/shard_map/psum | solution.py:163
  (51 shorter events, 8.5 us)
Async XLA Ops:
  8.0 86.5 %copy-start = (bf16[512,2048]{1,0:T(8,128)(2,1)S(1)}, bf16[512,2048]{1,0:T(8,128)(2,1)}, u32[]{:S(2)}) copy-start(bf16[512,2048]{1,0:T(8,128)(2,1)} %param.24) | copy-start | bytes 6291460
  8.0 126.1 %all-reduce.3.cloned.1.call-start = ((), (), s32[]{:S(2)}) async-start(), calls=%async_computation.1 | async-start | bytes 2097152 | tf_op jit(solution)/shard_map/psum | solution.py:128
  9.8 2.4 copy-start.4
  12.2 38.1 %copy-start.9 = (f32[256]{0:T(256)S(1)}, f32[256]{0:T(256)}, u32[]{:S(2)}) copy-start(f32[256]{0:T(256)} %param.23) | copy-start | bytes 3076
  12.6 72.4 %copy-start.8 = (f32[512]{0:T(512)S(1)}, f32[512]{0:T(512)}, u32[]{:S(2)}) copy-start(f32[512]{0:T(512)} %param.19) | copy-start | bytes 6148
  13.3 71.7 %copy-start.6 = (bf16[2048,512]{1,0:T(8,128)(2,1)S(1)}, bf16[2048,512]{1,0:T(8,128)(2,1)}, u32[]{:S(2)}) copy-start(bf16[2048,512]{1,0:T(8,128)(2,1)} %param.18) | copy-start | bytes 6291460
  87.8 2.6 copy-start.2
  90.5 1.0 copy-start.3
  96.2 38.0 %copy-start.1 = (bf16[2,128,2048]{2,1,0:T(8,128)(2,1)S(1)}, bf16[2,128,2048]{2,1,0:T(8,128)(2,1)}, u32[]{:S(2)}) copy-start(bf16[2,128,2048]{2,1,0:T(8,128)(2,1)} %param.16) | copy-start | bytes 3145732
  96.2 96.0 %all-gather.4.cloned.1.call-start = ((), (), s32[]{:S(2)}) async-start(), calls=%async_computation.2 | async-start | bytes 6488064 | tf_op jit(solution)/shard_map/all_gather | solution.py:134
  96.8 187.8 %all-gather.6.cloned.1.call-start = ((), (), s32[]{:S(2)}) async-start(), calls=%async_computation.3 | async-start | bytes 6488064 | tf_op jit(solution)/shard_map/all_gather | solution.py:139
  97.4 94.9 %copy-start.7 = (f32[2048]{0:T(1024)S(1)}, f32[2048]{0:T(1024)}, u32[]{:S(2)}) copy-start(f32[2048]{0:T(1024)} %param.25) | copy-start | bytes 24580
  97.4 279.5 %all-gather.8.cloned.1.call-start = ((), (), s32[]{:S(2)}) async-start(), calls=%async_computation.4 | async-start | bytes 6488064 | tf_op jit(solution)/shard_map/all_gather | solution.py:145
  97.9 311.6 %reduce-scatter.2.cloned.1.call-start = ((), (), s32[]{:S(2)}) async-start(), calls=%async_computation.5 | async-start | bytes 1310720 | tf_op jit(solution)/shard_map/reduce_scatter | solution.py:149
  386.4 30.7 %copy-start.5 = (s32[2]{0:T(128)S(1)}, s32[2]{0:T(128)}, u32[]{:S(2)}) copy-start(s32[2]{0:T(128)} %param.29) | copy-start | bytes 28
Sparse Core Ops, SparseCore 0:
  96.3 37.7 all-reduce.2
  386.6 22.9 reduce-scatter.1
Sparse Core Ops, SparseCore 1:
  98.9 93.3 all-gather.3
  194.3 90.2 all-gather.5
  286.6 90.2 all-gather.7
where the time goes:
time: 448 us; the launch traced here: 447 us
  waiting for transfers between devices  295 us (66%)
  blocking collectives  95.7 us (21%)
  matrix products  22.6 us (5%)
  between operations  15.9 us (4%)
  other arithmetic  15.5 us (3%)
    all_gather x1, waiting for transfers between devices, local(): lax.all_gather(down_weight, 'seq', axis=0, tiled=True)  92.4 us
    all_gather x1, waiting for transfers between devices, local(): lax.all_gather(up_weight, 'seq', axis=0, tiled=True)  86.4 us
    all_gather x1, waiting for transfers between devices, local(): lax.all_gather(gate_weight, 'seq', axis=0, tiled=True)  55.5 us
    psum x1, waiting for transfers between devices, local(): summed = lax.psum(projected.astype(jnp.bfloat16), 'mp').astype(jnp.float32)  35.9 us
    all_gather x1, blocking collectives, local(): key_piece = lax.all_gather(rotated_k, 'seq', axis=1, tiled=True)  35.3 us
    all_gather x1, blocking collectives, local(): value_piece = lax.all_gather(value_rows, 'seq', axis=1, tiled=True)  33.2 us
    reduce_scatter x1, waiting for transfers between devices, local(): lax.psum_scatter(down_part.astype(jnp.bfloat16), 'mp', scatter_dimension=...  23.1 us
    psum x1, blocking collectives, local(): seq_total = lax.psum(jnp.sum(influence, axis=1), 'seq')  21.5 us
  transfers between devices with their start and end apart: 5, of which 5 were waited for; matrix products, arithmetic and copies ran while one was open for 2% of the time, Pallas kernels for 0%

commit v1 on v0

--- a/solution.py
+++ b/solution.py
@@ -104,7 +104,12 @@
         )
     )
     key_start = jnp.int32(0)
-    key_piece = lax.all_gather(rotated_k, "seq", axis=1, tiled=True)
+    ring = [rotated_k]
+    for hop in range(7):
+        ring.append(lax.ppermute(ring[-1], "seq", [(dev, (dev + 1) % 8) for dev in range(8)]))
+    key_piece = jnp.roll(
+        jnp.concatenate(ring[::-1], axis=1), (lax.axis_index("seq") + 1) * ring[0].shape[1], axis=1
+    )
     value_piece = lax.all_gather(value_rows, "seq", axis=1, tiled=True)
     updated = []
     for state, query_entry in zip(initial, query_sets):

time: 448 us -> 462 us (1.031)
  blocking collectives: 95.7 us -> 58.9 us
  waiting for transfers between devices: 295 us -> 328 us
  local copies, waits for them, and re-layouts: 2.51 us -> 17.9 us
    all_gather x1 -> x0, blocking collectives: 35.3 us -> none  [local(): key_piece = lax.all_gather(rotated_k, 'seq', axis=1, tiled=True)]
    ppermute x0 -> x7, waiting for transfers between devices: none -> 33.5 us  [local(): lax.ppermute(ring[-1], 'seq', [(dev, (dev + 1) % 8) for dev in range(8)])]
    unnamed x18 -> x41, local copies, waits for them, and re-layouts: 0.05 us -> 12.9 us
  transfers between devices with their start and end apart: 5 -> 12, of which waited for: 5 -> 11; matrix products, arithmetic and copies ran while one was open for 2% -> 3% of each run, Pallas kernels for 0% -> 0%
where the time goes in v1:
time: 462 us
  waiting for transfers between devices  328 us (71%)
  blocking collectives  58.9 us (13%)
  matrix products  24.5 us (5%)
  local copies, waits for them, and re-layouts  17.9 us (4%)
  between operations  15.9 us (3%)
  other arithmetic  12.9 us (3%)
    all_gather x1, waiting for transfers between devices, local(): lax.all_gather(down_weight, 'seq', axis=0, tiled=True)  92.4 us
    all_gather x1, waiting for transfers between devices, local(): lax.all_gather(up_weight, 'seq', axis=0, tiled=True)  86.4 us
    all_gather x1, waiting for transfers between devices, local(): lax.all_gather(gate_weight, 'seq', axis=0, tiled=True)  55.5 us
    psum x1, waiting for transfers between devices, local(): summed = lax.psum(projected.astype(jnp.bfloat16), 'mp').astype(jnp.float32)  35.9 us
    ppermute x7, waiting for transfers between devices, local(): lax.ppermute(ring[-1], 'seq', [(dev, (dev + 1) % 8) for dev in range(8)])  33.5 us
    all_gather x1, blocking collectives, local(): value_piece = lax.all_gather(value_rows, 'seq', axis=1, tiled=True)  31.6 us
    reduce_scatter x1, waiting for transfers between devices, local(): lax.psum_scatter(down_part.astype(jnp.bfloat16), 'mp', scatter_dimension=...  23.1 us
    psum x1, blocking collectives, local(): seq_total = lax.psum(jnp.sum(influence, axis=1), 'seq')  21.5 us
  transfers between devices with their start and end apart: 12, of which 11 were waited for; matrix products, arithmetic and copies ran while one was open for 3% of the time, Pallas kernels for 0%

profile of v1, /device:TPU:0, one launch (start us, length us, event | category | flops | bytes accessed | tf_op | source)
XLA Modules:
  0.0 461.8 jit_solution(6945388479294936853)
XLA Ops:
  8.1 1.6 multiply_reduce_fusion
  14.9 3.1 collective-permute-start
  17.9 5.3 %collective-permute-done = bf16[2,128,128]{2,1,0:T(8,128)(2,1)S(1)} collective-permute-done((bf16[2,128,128]{2,1,0:T(8,128)(2,1)S(1)}, bf16[2,128,128]{2,1,0:T(8,128)(2,1)S(1)}, u32[]{:S(2)}, u32[]{:S(2)}) %collective-permute-start) | collective-permute-done | bytes 65568 | tf_op jit(solution)/shard_map/ppermute | solution.py:109
  23.2 7.0 %collective-permute-done.1 = bf16[2,128,128]{2,1,0:T(8,128)(2,1)S(1)} collective-permute-done((bf16[2,128,128]{2,1,0:T(8,128)(2,1)S(1)}, bf16[2,128,128]{2,1,0:T(8,128)(2,1)S(1)}, u32[]{:S(2)}, u32[]{:S(2)}) %collective-permute-start.1) | collective-permute-done | bytes 65568 | tf_op jit(solution)/shard_map/ppermute | solution.py:109
  30.2 3.1 convolution_add_fusion
  33.3 2.0 reshape.196
  37.4 6.7 %collective-permute-done.3 = bf16[2,128,128]{2,1,0:T(8,128)(2,1)S(1)} collective-permute-done((bf16[2,128,128]{2,1,0:T(8,128)(2,1)S(1)}, bf16[2,128,128]{2,1,0:T(8,128)(2,1)S(1)}, u32[]{:S(2)}, u32[]{:S(2)}) %collective-permute-start.3) | collective-permute-done | bytes 65568 | tf_op jit(solution)/shard_map/ppermute | solution.py:109
  44.6 6.5 %collective-permute-done.4 = bf16[2,128,128]{2,1,0:T(8,128)(2,1)S(1)} collective-permute-done((bf16[2,128,128]{2,1,0:T(8,128)(2,1)S(1)}, bf16[2,128,128]{2,1,0:T(8,128)(2,1)S(1)}, u32[]{:S(2)}, u32[]{:S(2)}) %collective-permute-start.4) | collective-permute-done | bytes 65568 | tf_op jit(solution)/shard_map/ppermute | solution.py:109
  51.3 7.4 %collective-permute-done.5 = bf16[2,128,128]{2,1,0:T(8,128)(2,1)S(1)} collective-permute-done((bf16[2,128,128]{2,1,0:T(8,128)(2,1)S(1)}, bf16[2,128,128]{2,1,0:T(8,128)(2,1)S(1)}, u32[]{:S(2)}, u32[]{:S(2)}) %collective-permute-start.5) | collective-permute-done | bytes 65568 | tf_op jit(solution)/shard_map/ppermute | solution.py:109
  58.8 31.6 %all_gather.12 = bf16[2,1024,128]{2,1,0:T(8,128)(2,1)S(1)} all-gather(bf16[2,128,128]{2,1,0:T(8,128)(2,1)S(1)} %bitcast.60), channel_id=1, replica_groups=mesh['seq'=8,'mp'=4] {'seq'}, dimensions={1}, use_global_device_ids=true | all-gather | bytes 589824 | tf_op jit(solution)/shard_map/all_gather | solution.py:113
  103.9 4.5 conditional.1
  104.0 1.9 fusion
  108.8 1.7 convolution_convert_fusion
  112.5 35.9 %all-reduce.3.cloned.1.call-done = bf16[256,2048]{1,0:T(8,128)(2,1)} async-done(((bf16[256,2048]{1,0:T(8,128)(2,1)}), bf16[256,2048]{1,0:T(8,128)(2,1)}) %all-reduce.3.cloned.1.call-update) | async-done | bytes 1048592 | tf_op jit(solution)/shard_map/psum | solution.py:133
  148.4 2.6 fusion.18
  151.0 55.5 %all-gather.4.cloned.1.call-done = bf16[2048,1408]{1,0:T(8,128)(2,1)} async-done(((bf16[256,1408]{1,0:T(8,128)(2,1)}), bf16[2048,1408]{1,0:T(8,128)(2,1)}) %all-gather.4.cloned.1.call-update) | async-done | bytes 5767184 | tf_op jit(solution)/shard_map/all_gather | solution.py:139
  206.5 6.0 %fusion.30 = f32[256,1408]{1,0:T(8,128)} fusion(bf16[2048,1408]{1,0:T(8,128)(2,1)} %all-gather.4.cloned.1.call-done, bf16[256,2048]{1,0:T(8,128)(2,1)} %get-tuple-element.138, f32[2048]{0:T(1024)S(1)} %copy-done.10, f32[256]{0:T(256)S(1)} %add_rsqrt_fusion), kind=kOutput, calls=%fused_computation.50 | convolution fusion | flops 1478492160 | bytes 8266752 | tf_op jit(solution)/shard_map/dot_general | solution.py:137
  212.5 86.4 %all-gather.6.cloned.1.call-done = bf16[2048,1408]{1,0:T(8,128)(2,1)} async-done(((bf16[256,1408]{1,0:T(8,128)(2,1)}), bf16[2048,1408]{1,0:T(8,128)(2,1)}) %all-gather.6.cloned.1.call-update) | async-done | bytes 5767184 | tf_op jit(solution)/shard_map/all_gather | solution.py:144
  298.9 92.4 %all-gather.8.cloned.1.call-done = bf16[2048,1408]{1,0:T(8,128)(2,1)} async-done(((bf16[256,1408]{1,0:T(8,128)(2,1)}), bf16[2048,1408]{1,0:T(8,128)(2,1)}) %all-gather.8.cloned.1.call-update) | async-done | bytes 5767184 | tf_op jit(solution)/shard_map/all_gather | solution.py:150
  391.2 9.5 %convolution_convert_fusion.1 = bf16[256,2048]{1,0:T(8,128)(2,1)} fusion(bf16[2048,1408]{1,0:T(8,128)(2,1)} %all-gather.8.cloned.1.call-done, bf16[2048,1408]{1,0:T(8,128)(2,1)} %all-gather.6.cloned.1.call-done, f32[256,1408]{1,0:T(8,128)} %fusion.30, bf16[256,2048]{1,0:T(8,128)(2,1)} %get-tuple-element.138, f32[2048]{0:T(1024)S(1)} %copy-done.10, ...), kind=kOutput, calls=%fused_computation.25 | convolution fusion | flops 2957574144 | bytes 15082496 | tf_op jit(solution)/shard_map/dot_general | solution.py:148
  400.8 23.1 %reduce-scatter.2.cloned.1.call-done = bf16[256,512]{1,0:T(8,128)(2,1)} async-done(((bf16[256,2048]{1,0:T(8,128)(2,1)}), bf16[256,512]{1,0:T(8,128)(2,1)}) %reduce-scatter.2.cloned.1.call-update) | async-done | bytes 262160 | tf_op jit(solution)/shard_map/reduce_scatter | solution.py:154
  423.9 1.8 fusion.23
  425.7 5.7 %all-reduce = (f32[2,128]{1,0:T(2,128)S(1)}, f32[2,128]{1,0:T(2,128)S(1)}) all-reduce(f32[2,128]{1,0:T(2,128)S(1)} %bitcast.63, f32[2,128]{1,0:T(2,128)S(1)} %bitcast.62), channel_id=1, replica_groups=mesh['seq'=8,'mp'=4] {'mp'}, use_global_device_ids=true, to_apply=%region_9.10 | all-reduce | flops 512 | bytes 4096 | tf_op jit(solution)/shard_map/psum | solution.py:162
  432.2 21.5 %psum.31 = f32[2]{0:T(128)S(1)} all-reduce(f32[2]{0:T(128)S(1)} %get-tuple-element.134), channel_id=1, replica_groups=mesh['seq'=8,'mp'=4] {'seq'}, use_global_device_ids=true, to_apply=%region_13.14 | all-reduce | flops 2 | bytes 16 | tf_op jit(solution)/shard_map/psum | solution.py:168
  (86 shorter events, 27.7 us)
Async XLA Ops:
  8.0 100.8 %copy-start = (bf16[512,2048]{1,0:T(8,128)(2,1)S(1)}, bf16[512,2048]{1,0:T(8,128)(2,1)}, u32[]{:S(2)}) copy-start(bf16[512,2048]{1,0:T(8,128)(2,1)} %param.24) | copy-start | bytes 6291460
  8.0 140.4 %all-reduce.3.cloned.1.call-start = ((), (), s32[]{:S(2)}) async-start(), calls=%async_computation.1 | async-start | bytes 2097152 | tf_op jit(solution)/shard_map/psum | solution.py:133
  10.6 19.6 %copy-start.11 = (f32[512]{0:T(512)S(1)}, f32[512]{0:T(512)}, u32[]{:S(2)}) copy-start(f32[512]{0:T(512)} %param.19) | copy-start | bytes 6148
  14.9 8.3 %collective-permute-start = (bf16[2,128,128]{2,1,0:T(8,128)(2,1)S(1)}, bf16[2,128,128]{2,1,0:T(8,128)(2,1)S(1)}, u32[]{:S(2)}, u32[]{:S(2)}) collective-permute-start(bf16[2,128,128]{2,1,0:T(8,128)(2,1)S(1)} %fusion.36), channel_id=1, source_target_pairs={{0,4},{4,8},{8,12},{12,16},{16,20},{20,24},{24,28},{28,0},{1,5},{5... | collective-permute-start | bytes 196616 | tf_op jit(solution)/shard_map/ppermute | solution.py:109
  23.2 7.0 %collective-permute-start.1 = (bf16[2,128,128]{2,1,0:T(8,128)(2,1)S(1)}, bf16[2,128,128]{2,1,0:T(8,128)(2,1)S(1)}, u32[]{:S(2)}, u32[]{:S(2)}) collective-permute-start(bf16[2,128,128]{2,1,0:T(8,128)(2,1)S(1)} %collective-permute-done), channel_id=1, source_target_pairs={{0,4},{4,8},{8,12},{12,16},{16,20},{20,24},{24,28},{28,0},{1,5},{5... | collective-permute-start | bytes 196616 | tf_op jit(solution)/shard_map/ppermute | solution.py:109
  30.2 7.0 %collective-permute-start.2 = (bf16[2,128,128]{2,1,0:T(8,128)(2,1)S(1)}, bf16[2,128,128]{2,1,0:T(8,128)(2,1)S(1)}, u32[]{:S(2)}, u32[]{:S(2)}) collective-permute-start(bf16[2,128,128]{2,1,0:T(8,128)(2,1)S(1)} %collective-permute-done.1), channel_id=1, source_target_pairs={{0,4},{4,8},{8,12},{12,16},{16,20},{20,24},{24,28},{28,0},{1,5},{5... | collective-permute-start | bytes 196616 | tf_op jit(solution)/shard_map/ppermute | solution.py:109
  33.3 4.1 copy-start.12
  35.3 8.8 %copy-start.8 = (bf16[2048,256]{1,0:T(8,128)(2,1)S(1)}, bf16[2048,256]{1,0:T(8,128)(2,1)}, u32[]{:S(2)}) copy-start(bf16[2048,256]{1,0:T(8,128)(2,1)} %param.22) | copy-start | bytes 3145732
  36.5 14.6 %copy-start.2 = (f32[2,128,4,128]{3,2,1,0:T(4,128)S(1)}, f32[2,128,4,128]{3,2,1,0:T(4,128)}, u32[]{:S(2)}) copy-start(f32[2,128,4,128]{3,2,1,0:T(4,128)} %reshape.196) | copy-start | bytes 1572868
  37.1 7.0 %copy-start.4 = (bf16[2,128,128]{2,1,0:T(8,128)(2,1)}, bf16[2,128,128]{2,1,0:T(8,128)(2,1)S(1)}, u32[]{:S(2)}) copy-start(bf16[2,128,128]{2,1,0:T(8,128)(2,1)S(1)} %collective-permute-done.2) | copy-start | bytes 196612
  37.1 7.0 %collective-permute-start.3 = (bf16[2,128,128]{2,1,0:T(8,128)(2,1)S(1)}, bf16[2,128,128]{2,1,0:T(8,128)(2,1)S(1)}, u32[]{:S(2)}, u32[]{:S(2)}) collective-permute-start(bf16[2,128,128]{2,1,0:T(8,128)(2,1)S(1)} %collective-permute-done.2), channel_id=1, source_target_pairs={{0,4},{4,8},{8,12},{12,16},{16,20},{20,24},{24,28},{28,0},{1,5},{5... | collective-permute-start | bytes 196616 | tf_op jit(solution)/shard_map/ppermute | solution.py:109
  44.1 14.6 %copy-start.6 = (bf16[2,128,128]{2,1,0:T(8,128)(2,1)}, bf16[2,128,128]{2,1,0:T(8,128)(2,1)S(1)}, u32[]{:S(2)}) copy-start(bf16[2,128,128]{2,1,0:T(8,128)(2,1)S(1)} %collective-permute-done.3) | copy-start | bytes 196612
  44.1 7.0 %collective-permute-start.4 = (bf16[2,128,128]{2,1,0:T(8,128)(2,1)S(1)}, bf16[2,128,128]{2,1,0:T(8,128)(2,1)S(1)}, u32[]{:S(2)}, u32[]{:S(2)}) collective-permute-start(bf16[2,128,128]{2,1,0:T(8,128)(2,1)S(1)} %collective-permute-done.3), channel_id=1, source_target_pairs={{0,4},{4,8},{8,12},{12,16},{16,20},{20,24},{24,28},{28,0},{1,5},{5... | collective-permute-start | bytes 196616 | tf_op jit(solution)/shard_map/ppermute | solution.py:109
  44.6 50.0 %copy-start.5 = (bf16[2,128,128]{2,1,0:T(8,128)(2,1)S(1)}, bf16[2,128,128]{2,1,0:T(8,128)(2,1)}, u32[]{:S(2)}) copy-start(bf16[2,128,128]{2,1,0:T(8,128)(2,1)} %copy-done.4) | copy-start | bytes 196612
  51.1 7.7 %copy-start.7 = (bf16[2,128,128]{2,1,0:T(8,128)(2,1)}, bf16[2,128,128]{2,1,0:T(8,128)(2,1)S(1)}, u32[]{:S(2)}) copy-start(bf16[2,128,128]{2,1,0:T(8,128)(2,1)S(1)} %collective-permute-done.4) | copy-start | bytes 196612
  51.1 7.7 %collective-permute-start.5 = (bf16[2,128,128]{2,1,0:T(8,128)(2,1)S(1)}, bf16[2,128,128]{2,1,0:T(8,128)(2,1)S(1)}, u32[]{:S(2)}, u32[]{:S(2)}) collective-permute-start(bf16[2,128,128]{2,1,0:T(8,128)(2,1)S(1)} %collective-permute-done.4), channel_id=1, source_target_pairs={{0,4},{4,8},{8,12},{12,16},{16,20},{20,24},{24,28},{28,0},{1,5},{5... | collective-permute-start | bytes 196616 | tf_op jit(solution)/shard_map/ppermute | solution.py:109
  58.7 31.6 %collective-permute-start.6 = (bf16[2,128,128]{2,1,0:T(8,128)(2,1)S(1)}, bf16[2,128,128]{2,1,0:T(8,128)(2,1)S(1)}, u32[]{:S(2)}, u32[]{:S(2)}) collective-permute-start(bf16[2,128,128]{2,1,0:T(8,128)(2,1)S(1)} %collective-permute-done.5), channel_id=1, source_target_pairs={{0,4},{4,8},{8,12},{12,16},{16,20},{20,24},{24,28},{28,0},{1,5},{5... | collective-permute-start | bytes 196616 | tf_op jit(solution)/shard_map/ppermute | solution.py:109
  110.5 37.9 %copy-start.1 = (bf16[2,128,2048]{2,1,0:T(8,128)(2,1)S(1)}, bf16[2,128,2048]{2,1,0:T(8,128)(2,1)}, u32[]{:S(2)}) copy-start(bf16[2,128,2048]{2,1,0:T(8,128)(2,1)} %param.16) | copy-start | bytes 3145732
  110.5 96.0 %all-gather.4.cloned.1.call-start = ((), (), s32[]{:S(2)}) async-start(), calls=%async_computation.2 | async-start | bytes 6488064 | tf_op jit(solution)/shard_map/all_gather | solution.py:139
  111.1 187.8 %all-gather.6.cloned.1.call-start = ((), (), s32[]{:S(2)}) async-start(), calls=%async_computation.3 | async-start | bytes 6488064 | tf_op jit(solution)/shard_map/all_gather | solution.py:144
  111.7 94.8 %copy-start.10 = (f32[2048]{0:T(1024)S(1)}, f32[2048]{0:T(1024)}, u32[]{:S(2)}) copy-start(f32[2048]{0:T(1024)} %param.25) | copy-start | bytes 24580
  111.7 279.5 %all-gather.8.cloned.1.call-start = ((), (), s32[]{:S(2)}) async-start(), calls=%async_computation.4 | async-start | bytes 6488064 | tf_op jit(solution)/shard_map/all_gather | solution.py:150
  112.3 311.6 %reduce-scatter.2.cloned.1.call-start = ((), (), s32[]{:S(2)}) async-start(), calls=%async_computation.5 | async-start | bytes 1310720 | tf_op jit(solution)/shard_map/reduce_scatter | solution.py:154
  400.8 30.7 %copy-start.9 = (s32[2]{0:T(128)S(1)}, s32[2]{0:T(128)}, u32[]{:S(2)}) copy-start(s32[2]{0:T(128)} %param.29) | copy-start | bytes 28
  (1 other events, 2.4 us)
Sparse Core Ops, SparseCore 0:
  110.7 37.7 all-reduce.2
  400.9 22.9 reduce-scatter.1
Sparse Core Ops, SparseCore 1:
  113.2 93.2 all-gather.3
  208.6 90.2 all-gather.5
  300.9 90.2 all-gather.7
